TPU v7x, 32 devices: a whole 2x2x4 slice. The times are simulated.
32 devices in a mesh: row: 4 (over y, x), col: 8 (over z, core).
Axes of the slice: x: 2, y: 2, z: 4, core: 2. Of those that a mesh axis runs over, the one named last changes fastest.
Arguments:
- inputs: bfloat16 [256, 16384], P('col', 'row'), may hold values from -0.375 to 0.375
- weight: bfloat16 [16384, 18432], P('row', 'col'), may hold values from -0.046875 to 0.046875
- grad_out: bfloat16 [256, 18432], P('row', 'col'), may hold values from -6 to 6
- positions: int32 [256], P('row'), may hold values from 0 to 8191
Outputs:
- input_grad: bfloat16 [256, 16384], P('col', 'row')
- weight_grad: float32 [16384, 18432], P('row', 'col')
All inputs are finite; a program needn't handle non-finite values.
Results may differ from a plain program's by a relative error of at most 0.0065.
Values may be sent and summed in bfloat16 or wider, within the bound.
A program may use at most 192 MiB of HBM per device.

v0:
```python
import functools
import math

import jax
import jax.numpy as jnp
from jax import lax
from jax.experimental import pallas as pl
from jax.experimental.pallas import tpu as pltpu
from jax.sharding import PartitionSpec as P

QHEADS = 128
KVHEADS = 8
HEAD = 128
PAIR_LAG = 2
LEVEL_LAG = 3
MESH = pl.DeviceIdType.MESH


def scaled_freq(within):
    base = jnp.exp(-(2.0 * within.astype(jnp.float32) / HEAD) * math.log(500000.0))
    wave = 2.0 * math.pi / base
    smooth = (8192.0 / wave - 1.0) / 3.0
    middle = (1.0 - smooth) * base / 8.0 + smooth * base
    return jnp.where(wave < 2048.0, base, jnp.where(wave > 8192.0, base / 8.0, middle))


def unrotate(grad, positions, col_start):
    width = grad.shape[1]
    lanes = col_start + jnp.arange(HEAD, dtype=jnp.int32)
    freq = scaled_freq(lanes % HEAD // 2)
    angle = positions.astype(jnp.float32)[:, None] * freq[None, :]
    cosine = jnp.cos(angle)
    sine = jnp.where((lanes % 2 == 0)[None, :], jnp.sin(angle), -jnp.sin(angle))
    reps = -(-width // HEAD)
    cosine = jnp.tile(cosine, (1, reps))[:, :width]
    sine = jnp.tile(sine, (1, reps))[:, :width]
    columns = col_start + jnp.arange(width, dtype=jnp.int32)
    rotated = (columns < (QHEADS + KVHEADS) * HEAD)[None, :]
    wide = grad.astype(jnp.float32)
    other = jnp.where(
        (columns % 2 == 0)[None, :], jnp.roll(wide, -1, axis=1), jnp.roll(wide, 1, axis=1)
    )
    return jnp.where(rotated, wide * cosine + other * sine, wide).astype(jnp.bfloat16)


def unrotate_heads(g_ref, pos_ref, out, col_start):
    trow, width = g_ref.shape
    lanes = col_start + lax.broadcasted_iota(jnp.int32, (trow, HEAD), 1)
    freq = scaled_freq((col_start + lax.broadcasted_iota(jnp.int32, (8, HEAD), 1)) % HEAD // 2)[0:1, :]
    row = lax.broadcasted_iota(jnp.int32, (trow, trow), 0)
    lane = lax.broadcasted_iota(jnp.int32, (trow, trow), 1)
    spread = jnp.broadcast_to(pos_ref[...].astype(jnp.float32), (trow, trow))
    column = jnp.sum(jnp.where(row == lane, spread, 0.0), axis=1, keepdims=True)
    angle = column * freq
    even = lanes % 2 == 0
    cosine = jnp.cos(angle)
    sine = jnp.sin(angle)
    sine = jnp.where(even, sine, -sine)
    for first in range(0, width, HEAD):
        wide = g_ref[:, first:first + HEAD].astype(jnp.float32)
        other = jnp.where(even, pltpu.roll(wide, HEAD - 1, 1), pltpu.roll(wide, 1, 1))
        turned = wide * cosine + other * sine
        rotated = lanes + first < (QHEADS + KVHEADS) * HEAD
        out[0:trow, first:first + HEAD] = jnp.where(rotated, turned, wide).astype(jnp.bfloat16)


def exclusive_or(a, b, size):
    total, bit = 0, 1
    while bit < size:
        total = total + bit * ((a // bit % 2 + b // bit % 2) % 2)
        bit *= 2
    return total


def kernel(rows_n, chips, parts, raw, g_ref, pos_ref, x_ref, w_ref, gall, xall, out_ref,
           w_v, pb, rb, ub, db, sb_up, sb_dn,
           w_sem, gs, gr, xs_up, xs_dn, xs_p, xr, xp, ps, pr, us, ur, ds, dr):
    r = lax.axis_index("row")
    q = lax.axis_index("col")
    z, c = q // 2, q % 2
    mate = z * 2 + 1 - c
    up, down = q + 2, q - 2
    trow, tcol = g_ref.shape[0], x_ref.shape[0]
    depth = w_ref.shape[0]
    dc = depth // parts

    def w_copy(h):
        rows = pl.ds(h * dc, dc)
        return pltpu.make_async_copy(w_ref.at[rows], w_v.at[rows], w_sem.at[h])

    for h in range(parts):
        w_copy(h).start()

    if raw:
        unrotate_heads(g_ref, pos_ref, gall, q * g_ref.shape[1])
    else:
        gall[0:trow, :] = g_ref[...]

    barrier = pltpu.get_barrier_semaphore()
    for j in range(1, rows_n):
        pl.semaphore_signal(barrier, inc=1, device_id=(exclusive_or(r, j, rows_n), q), device_id_type=MESH)
    pl.semaphore_signal(barrier, inc=1, device_id=(r, mate), device_id_type=MESH)

    @pl.when(z > 0)
    def _():
        pl.semaphore_signal(barrier, inc=1, device_id=(r, down), device_id_type=MESH)

    @pl.when(z < chips - 1)
    def _():
        pl.semaphore_signal(barrier, inc=1, device_id=(r, up), device_id_type=MESH)

    inner = (z > 0) & (z < chips - 1)

    @pl.when(inner)
    def _():
        pl.semaphore_wait(barrier, rows_n + 2)

    @pl.when(jnp.logical_not(inner))
    def _():
        pl.semaphore_wait(barrier, rows_n + 1)

    def send(src, dst, s_sem, r_sem, row, col):
        return pltpu.make_async_remote_copy(
            src_ref=src, dst_ref=dst, send_sem=s_sem, recv_sem=r_sem,
            device_id=(row, col), device_id_type=MESH,
        )

    width = g_ref.shape[1]
    relayed = rows_n == 4 and width % 256 == 0
    cut = width // 2 if relayed else width
    halves = (slice(0, cut), slice(cut, width)) if relayed else (slice(0, width),)

    def g_copy(j, k):
        return send(gall.at[0:trow, halves[k]], gall.at[j * trow:(j + 1) * trow, halves[k]],
                    gs.at[j, k], gr.at[j, k], exclusive_or(r, j, rows_n), q)

    def g_relay(j):
        k = j - 1
        return send(gall.at[j * trow:(j + 1) * trow, halves[k]], gall.at[3 * trow:4 * trow, halves[k]],
                    gs.at[3, k], gr.at[3, k], exclusive_or(r, 3 - j, rows_n), q)

    if relayed:
        first = [g_copy(1, 0), g_copy(2, 1), g_copy(1, 1), g_copy(2, 0)]
        second = [g_relay(1), g_relay(2)]
    else:
        first = [g_copy(j, 0) for j in range(1, rows_n)]
        second = []
    for copy in first:
        copy.start()

    def x_rows(chip, core):
        return pl.ds(pl.multiple_of(exclusive_or(r, chip, chips) * (2 * tcol) + core * tcol, tcol), tcol)

    own = xall.at[x_rows(z, c)]
    own_up = send(x_ref, own, xs_up.at[z], xr.at[z], r, up)
    own_dn = send(x_ref, own, xs_dn.at[z], xr.at[z], r, down)
    own_p = send(x_ref, own, xs_p.at[z], xp.at[z], r, mate)

    @pl.when(z < chips - 1)
    def _():
        own_up.start()

    @pl.when(z > 0)
    def _():
        own_dn.start()

    own_p.start()
    xall[x_rows(z, c), :] = x_ref[...]

    def block_copies(chip):
        block = xall.at[x_rows(chip, c)]
        return (send(block, block, xs_up.at[chip], xr.at[chip], r, up),
                send(block, block, xs_dn.at[chip], xr.at[chip], r, down),
                send(block, block, xs_p.at[chip], xp.at[chip], r, mate))

    def forward(distance):
        @pl.when(z >= distance)
        def _():
            to_up, _unused, to_mate = block_copies(z - distance)
            to_up.wait_recv()

            @pl.when(z < chips - 1)
            def _():
                to_up.start()

            to_mate.start()

        @pl.when(z + distance < chips)
        def _():
            _unused, to_dn, to_mate = block_copies(z + distance)
            to_dn.wait_recv()

            @pl.when(z > 0)
            def _():
                to_dn.start()

            to_mate.start()

    def part(h):
        return pl.ds(pl.multiple_of(h * dc, dc), dc)

    def pair_copy(h):
        return send(pb.at[1 - c, :, :, part(h)], rb.at[:, :, part(h)], ps.at[h], pr.at[h], r, mate)

    def pair_sum(b, h):
        j = exclusive_or(r, b, rows_n)
        return pb[c, j, :, part(h)].astype(jnp.float32) + rb[j, :, part(h)].astype(jnp.float32)

    def up_copy(b, h):
        return send(sb_up.at[b, :, part(h)], ub.at[b, :, part(h)], us.at[b, h], ur.at[b, h], r, up)

    def dn_copy(b, h):
        return send(sb_dn.at[b, :, part(h)], db.at[b, :, part(h)], ds.at[b, h], dr.at[b, h], r, down)

    def up_step(h):
        def body(i, carry):
            b = chips - 1 - i
            copy = up_copy(b, h)

            @pl.when(z == 0)
            def _():
                sb_up[b, :, part(h)] = pair_sum(b, h).astype(jnp.bfloat16)

            @pl.when(z > 0)
            def _():
                copy.wait_recv()
                sb_up[b, :, part(h)] = (pair_sum(b, h) + ub[b, :, part(h)].astype(jnp.float32)).astype(jnp.bfloat16)

            copy.start()
            return carry

        lax.fori_loop(0, chips - 1 - z, body, 0)

    def dn_step(h):
        def body(b, carry):
            copy = dn_copy(b, h)

            @pl.when(z == chips - 1)
            def _():
                sb_dn[b, :, part(h)] = pair_sum(b, h).astype(jnp.bfloat16)

            @pl.when(z < chips - 1)
            def _():
                copy.wait_recv()
                sb_dn[b, :, part(h)] = (pair_sum(b, h) + db[b, :, part(h)].astype(jnp.float32)).astype(jnp.bfloat16)

            copy.start()
            return carry

        lax.fori_loop(0, z, body, 0)

    def final_step(h):
        total = pair_sum(z, h)

        @pl.when(z > 0)
        def _():
            up_copy(z, h).wait_recv()

        @pl.when(z < chips - 1)
        def _():
            dn_copy(z, h).wait_recv()

        @pl.when(z == 0)
        def _():
            out_ref[:, part(h)] = (total + db[z, :, part(h)].astype(jnp.float32)).astype(jnp.bfloat16)

        @pl.when(z == chips - 1)
        def _():
            out_ref[:, part(h)] = (total + ub[z, :, part(h)].astype(jnp.float32)).astype(jnp.bfloat16)

        @pl.when((z > 0) & (z < chips - 1))
        def _():
            out_ref[:, part(h)] = (total + ub[z, :, part(h)].astype(jnp.float32)
                                   + db[z, :, part(h)].astype(jnp.float32)).astype(jnp.bfloat16)

    tile = min(dc, 512)

    def multiply(h):
        w_copy(h).wait()

        def body(t, carry):
            at = pl.multiple_of(h * dc + t * tile, tile)
            product = lax.dot_general(
                w_v[pl.ds(at, tile), :], gall[...], (((1,), (1,)), ((), ())),
                preferred_element_type=jnp.float32,
            )
            flat = product.T.astype(jnp.bfloat16)
            for j in range(rows_n):
                for core in range(2):
                    first = j * trow + core * tcol
                    pb[core, j, :, pl.ds(at, tile)] = flat[first:first + tcol, :]
            return carry

        lax.fori_loop(0, dc // tile, body, 0)
        pair_copy(h).start()

    for copy, relay in zip(first, second):
        copy.wait_recv()
        relay.start()
    forward(1)
    for copy in first[len(second):] + second:
        copy.wait_recv()

    last = PAIR_LAG + LEVEL_LAG * (chips - 1)
    for slot in range(parts + last):
        if slot < parts:
            multiply(slot)
        if 0 <= slot - PAIR_LAG < parts:
            pair_copy(slot - PAIR_LAG).wait_recv()
        h_up = slot - PAIR_LAG - LEVEL_LAG * z
        h_dn = slot - PAIR_LAG - LEVEL_LAG * (chips - 1 - z)

        @pl.when((h_up >= 0) & (h_up < parts))
        def _():
            up_step(h_up)

        @pl.when((h_dn >= 0) & (h_dn < parts))
        def _():
            dn_step(h_dn)

        if 0 <= slot - last < parts:
            final_step(slot - last)
        if slot == parts // 4:
            for distance in range(2, chips - 1):
                forward(distance)
    if chips > 2:
        forward(chips - 1)

    for copy in first + second:
        copy.wait_send()
    for h in range(parts):
        pair_copy(h).wait_send()
    for chip in range(chips):
        to_up, to_dn, to_mate = block_copies(chip)
        to_mate.wait()

        @pl.when((z >= chip) & (z < chips - 1))
        def _():
            to_up.wait_send()

        @pl.when((z <= chip) & (z > 0))
        def _():
            to_dn.wait_send()

        for h in range(parts):
            @pl.when(z < chip)
            def _():
                up_copy(chip, h).wait_send()

            @pl.when(z > chip)
            def _():
                dn_copy(chip, h).wait_send()


def outer_sum(left, right):
    return lax.dot_general(
        left, right, (((0,), (0,)), ((), ())), preferred_element_type=jnp.float32
    )


def per_device(rows_n, chips, inputs, weight, grad_out, positions):
    depth, width = weight.shape
    trow, tcol = grad_out.shape[0], inputs.shape[0]
    col_start = lax.axis_index("col") * width
    raw = width % HEAD == 0
    grad = grad_out if raw else unrotate(grad_out, positions, col_start)
    parts = 8 if depth % (8 * HEAD) == 0 else 4
    dma = pltpu.SemaphoreType.DMA
    vmem = pl.BlockSpec(memory_space=pltpu.VMEM)
    half = jnp.bfloat16
    whole_grad, whole_inputs, input_grad = pl.pallas_call(
        functools.partial(kernel, rows_n, chips, parts, raw),
        out_shape=(
            jax.ShapeDtypeStruct((rows_n * trow, width), half),
            jax.ShapeDtypeStruct((chips * 2 * tcol, depth), half),
            jax.ShapeDtypeStruct((tcol, depth), half),
        ),
        in_specs=[vmem, vmem, vmem, pl.BlockSpec(memory_space=pl.ANY)],
        out_specs=(vmem, vmem, vmem),
        scratch_shapes=[
            pltpu.VMEM((depth, width), half),
            pltpu.VMEM((2, rows_n, tcol, depth), half),
            pltpu.VMEM((rows_n, tcol, depth), half),
            pltpu.VMEM((chips, tcol, depth), half),
            pltpu.VMEM((chips, tcol, depth), half),
            pltpu.VMEM((chips, tcol, depth), half),
            pltpu.VMEM((chips, tcol, depth), half),
            dma((parts,)),
            dma((rows_n, 2)), dma((rows_n, 2)),
            dma((chips,)), dma((chips,)), dma((chips,)), dma((chips,)), dma((chips,)),
            dma((parts,)), dma((parts,)),
            dma((chips, parts)), dma((chips, parts)), dma((chips, parts)), dma((chips, parts)),
        ],
        compiler_params=pltpu.CompilerParams(
            collective_id=0, has_side_effects=True, vmem_limit_bytes=60 * 2**20
        ),
        cost_estimate=pl.CostEstimate(
            flops=2 * rows_n * trow * width * depth, bytes_accessed=2 * width * depth, transcendentals=0
        ),
    )(grad, positions[None, :], inputs, weight)
    weight_grad = outer_sum(whole_inputs, whole_grad)
    return (input_grad, weight_grad)


def solution(mesh):
    rows_n, chips = mesh.shape["row"], mesh.shape["col"] // 2
    in_specs = (P("col", "row"), P("row", "col"), P("row", "col"), P("row"))
    out_specs = (P("col", "row"), P("row", "col"))
    return jax.shard_map(
        functools.partial(per_device, rows_n, chips), mesh=mesh, in_specs=in_specs,
        out_specs=out_specs, check_vma=False,
    )
```

profile of v0, /device:TPU:0, one launch (start us, length us, event | category | flops | bytes accessed | tf_op | source)
XLA Modules:
  0.0 68.8 jit_solution(13113008576532090548)
XLA Ops:
  0.6 50.1 %shard_map.59 = (bf16[256,2304]{1,0:T(8,128)(2,1)}, bf16[256,4096]{1,0:T(8,128)(2,1)}, bf16[32,4096]{1,0:T(8,128)(2,1)}) custom-call(bf16[64,2304]{1,0:T(8,128)(2,1)} %g_ref.1, s32[1,64]{1,0:T(1,128)} %bitcast.3, bf16[32,4096]{1,0:T(8,128)(2,1)} %x_ref.1, bf16[4096,2304]{1,0:T(8,128)(2,1)} %w_ref.1), custom_call_target="tpu_custom_call" | custom-call | flops 4831838208 | bytes 18874368 | tf_op jit(solution)/shard_map/pallas_call | solution.py:371
  50.7 0.0 copy-start
  50.7 17.4 %fusion = f32[4096,2304]{1,0:T(8,128)} fusion(bf16[256,4096]{1,0:T(8,128)(2,1)} %get-tuple-element.6, bf16[256,2304]{1,0:T(8,128)(2,1)} %get-tuple-element.7), kind=kOutput, calls=%fused_computation | convolution fusion | flops 4831838208 | bytes 41025536 | tf_op jit(solution)/shard_map/dot_general | solution.py:356
  68.1 0.0 copy-done
  68.1 0.7 %copy.7 = bf16[32,4096]{1,0:T(8,128)(2,1)} copy(bf16[32,4096]{1,0:T(8,128)(2,1)S(1)} %copy-done) | data formatting | bytes 524288
Async XLA Ops:
  50.7 17.4 %copy-start = (bf16[32,4096]{1,0:T(8,128)(2,1)S(1)}, bf16[32,4096]{1,0:T(8,128)(2,1)}, u32[]{:S(2)}) copy-start(bf16[32,4096]{1,0:T(8,128)(2,1)} %get-tuple-element.10) | copy-start | bytes 786436
where the time goes:
time: 68.9 us; the launch traced here: 68.8 us
  Pallas kernels  50.1 us (73%)
  matrix products  17.4 us (25%)
  local copies, waits for them, and re-layouts  0.71 us (1%)
    pallas_call x1, Pallas kernels, per_device(): pl.pallas_call(functools.partial(kernel, rows_n, chips, parts, raw), out_...  50.1 us
    dot_general x1, matrix products, outer_sum(): lax.dot_general(left, right, (((0,), (0,)), ((), ())), preferred_element_...  17.4 us

commit v1 on v0

--- a/solution.py
+++ b/solution.py
@@ -14,6 +14,7 @@
 PAIR_LAG = 2
 LEVEL_LAG = 3
 MESH = pl.DeviceIdType.MESH
+half = jnp.bfloat16
 
 
 def scaled_freq(within):
@@ -352,6 +353,399 @@
                 dn_copy(chip, h).wait_send()
 
 
+def staged_kernel(rows_n, chips, parts, g_hbm, pos_ref, x_hbm, w_ref, gall, xall, own_ref, up_ref, dn_ref,
+                  w_v, raw, pb, rb, ub, db, sb_up, sb_dn,
+                  w_sem, in_sem, gs, gr, xs_up, xs_dn, xs_p, xr, xp, ps, pr, us, ur, ds, dr):
+    r = lax.axis_index("row")
+    q = lax.axis_index("col")
+    z, c = q // 2, q % 2
+    mate = z * 2 + 1 - c
+    up, down = q + 2, q - 2
+    trow, width = g_hbm.shape
+    tcol, depth = x_hbm.shape
+    dc = depth // parts
+    pieces = 2
+    prow = tcol // pieces
+
+    def x_rows(chip, core, p):
+        first = exclusive_or(r, chip, chips) * (2 * tcol) + core * tcol + p * prow
+        return pl.ds(pl.multiple_of(first, prow), prow)
+
+    g_in = pltpu.make_async_copy(g_hbm, raw, in_sem.at[0])
+    g_in.start()
+    x_in = [pltpu.make_async_copy(x_hbm.at[pl.ds(p * prow, prow)], xall.at[x_rows(z, c, p)], in_sem.at[1 + p])
+            for p in range(pieces)]
+    for copy in x_in:
+        copy.start()
+
+    barrier = pltpu.get_barrier_semaphore()
+    for j in (1, 2):
+        pl.semaphore_signal(barrier, inc=1, device_id=(exclusive_or(r, j, rows_n), q), device_id_type=MESH)
+    pl.semaphore_signal(barrier, inc=1, device_id=(r, mate), device_id_type=MESH)
+
+    @pl.when(z > 0)
+    def _():
+        pl.semaphore_signal(barrier, inc=1, device_id=(r, down), device_id_type=MESH)
+
+    @pl.when(z < chips - 1)
+    def _():
+        pl.semaphore_signal(barrier, inc=1, device_id=(r, up), device_id_type=MESH)
+
+    def w_copy(h):
+        rows = pl.ds(pl.multiple_of(h * dc, dc), dc)
+        return pltpu.make_async_copy(w_ref.at[rows], w_v.at[rows], w_sem.at[h])
+
+    for h in range(parts):
+        w_copy(h).start()
+
+    g_in.wait()
+    unrotate_heads(raw, pos_ref, gall, q * width)
+    for copy in x_in:
+        copy.wait()
+
+    inner = (z > 0) & (z < chips - 1)
+
+    @pl.when(inner)
+    def _():
+        pl.semaphore_wait(barrier, 5)
+
+    @pl.when(jnp.logical_not(inner))
+    def _():
+        pl.semaphore_wait(barrier, 4)
+
+    def send(src, dst, s_sem, r_sem, row, col):
+        return pltpu.make_async_remote_copy(
+            src_ref=src, dst_ref=dst, send_sem=s_sem, recv_sem=r_sem,
+            device_id=(row, col), device_id_type=MESH,
+        )
+
+    cut = width // 2
+    halves = (slice(0, cut), slice(cut, width))
+
+    def g_copy(j, k):
+        return send(gall.at[0:trow, halves[k]], gall.at[j * trow:(j + 1) * trow, halves[k]],
+                    gs.at[j, k], gr.at[j, k], exclusive_or(r, j, rows_n), q)
+
+    def g_relay(j):
+        k = j - 1
+        return send(gall.at[j * trow:(j + 1) * trow, halves[k]], gall.at[3 * trow:4 * trow, halves[k]],
+                    gs.at[3, k], gr.at[3, k], exclusive_or(r, 3 - j, rows_n), q)
+
+    g_first = [g_copy(1, 0), g_copy(2, 1)]
+    g_second = [g_copy(1, 1), g_copy(2, 0)]
+    g_third = [g_relay(1), g_relay(2)]
+    for copy in g_first + g_second:
+        copy.start()
+
+    def block_copies(chip, p):
+        block = xall.at[x_rows(chip, c, p)]
+        return (send(block, block, xs_up.at[chip, p], xr.at[chip, p], r, up),
+                send(block, block, xs_dn.at[chip, p], xr.at[chip, p], r, down),
+                send(block, block, xs_p.at[chip, p], xp.at[chip, p], r, mate))
+
+    for p in range(pieces):
+        to_up, to_dn, to_mate = block_copies(z, p)
+
+        @pl.when(z < chips - 1)
+        def _():
+            to_up.start()
+
+        @pl.when(z > 0)
+        def _():
+            to_dn.start()
+
+        to_mate.start()
+
+    def forward(distance, p):
+        @pl.when(z >= distance)
+        def _():
+            to_up, _unused, to_mate = block_copies(z - distance, p)
+            to_up.wait_recv()
+
+            @pl.when(z < chips - 1)
+            def _():
+                to_up.start()
+
+            to_mate.start()
+
+        @pl.when(z + distance < chips)
+        def _():
+            _unused, to_dn, to_mate = block_copies(z + distance, p)
+            to_dn.wait_recv()
+
+            @pl.when(z > 0)
+            def _():
+                to_dn.start()
+
+            to_mate.start()
+
+    def part(h):
+        return pl.ds(pl.multiple_of(h * dc, dc), dc)
+
+    def pair_copy(j, h):
+        return send(pb.at[1 - c, j, :, part(h)], rb.at[j, :, part(h)], ps.at[j, h], pr.at[j, h], r, mate)
+
+    def pair_sum(j, h):
+        return pb[c, j, :, part(h)].astype(jnp.float32) + rb[j, :, part(h)].astype(jnp.float32)
+
+    def up_copy(j, h):
+        return send(sb_up.at[j, :, part(h)], ub.at[j, :, part(h)], us.at[j, h], ur.at[j, h], r, up)
+
+    def dn_copy(j, h):
+        return send(sb_dn.at[j, :, part(h)], db.at[j, :, part(h)], ds.at[j, h], dr.at[j, h], r, down)
+
+    def multiply(i, first, last):
+        h = i % parts
+        product = lax.dot_general(
+            w_v[part(h), :], gall[first * trow:last * trow, :], (((1,), (1,)), ((), ())),
+            preferred_element_type=jnp.float32,
+        )
+        flat = product.T.astype(half)
+        for j in range(first, last):
+            for core in range(2):
+                at = (j - first) * trow + core * tcol
+                pb[core, j, :, part(h)] = flat[at:at + tcol, :]
+        for j in range(first, last):
+            pair_copy(j, h).start()
+
+    def each_block(i, act):
+        def body(j, carry):
+            least = parts * ((j + 3) // 4) + (parts // 2) * (j // 3)
+
+            @pl.when((i >= least) & (i < least + parts))
+            def _():
+                act(j, (i + 4 * LEVEL_LAG * parts) % parts, exclusive_or(r, j, rows_n))
+
+            return carry
+
+        lax.fori_loop(0, rows_n, body, 0)
+
+    def own_step(j, h, dest):
+        pair_copy(j, h).wait_recv()
+
+        @pl.when(dest == z)
+        def _():
+            own_ref[:, part(h)] = pair_sum(j, h)
+
+    def up_step(j, h, dest):
+        copy = up_copy(j, h)
+
+        def finish(total):
+            @pl.when(dest == z + 1)
+            def _():
+                up_ref[:, part(h)] = total.astype(half)
+
+            @pl.when(dest > z + 1)
+            def _():
+                sb_up[j, :, part(h)] = total.astype(half)
+                copy.start()
+
+        @pl.when((dest > z) & (z == 0))
+        def _():
+            finish(pair_sum(j, h))
+
+        @pl.when((dest > z) & (z > 0))
+        def _():
+            copy.wait_recv()
+            finish(pair_sum(j, h) + ub[j, :, part(h)].astype(jnp.float32))
+
+    def dn_step(j, h, dest):
+        copy = dn_copy(j, h)
+
+        def finish(total):
+            @pl.when(dest == z - 1)
+            def _():
+                dn_ref[:, part(h)] = total.astype(half)
+
+            @pl.when(dest < z - 1)
+            def _():
+                sb_dn[j, :, part(h)] = total.astype(half)
+                copy.start()
+
+        @pl.when((dest < z) & (z == chips - 1))
+        def _():
+            finish(pair_sum(j, h))
+
+        @pl.when((dest < z) & (z < chips - 1))
+        def _():
+            copy.wait_recv()
+            finish(pair_sum(j, h) + db[j, :, part(h)].astype(jnp.float32))
+
+    def settle(slot):
+        each_block(slot - 1, own_step)
+        each_block(slot - 1 - LEVEL_LAG * z, up_step)
+        each_block(slot - 1 - LEVEL_LAG * (chips - 1 - z), dn_step)
+
+    def products(start, stop, first, last, after):
+        def body(i, carry):
+            if start == 0:
+                w_copy(i).wait()
+            multiply(i, first, last)
+            for at, act in after:
+                pl.when(i == at)(act)
+            settle(i)
+            return carry
+
+        lax.fori_loop(start, stop, body, 0)
+
+    def early():
+        for copy, relay in zip(g_first, g_third):
+            copy.wait_recv()
+            relay.start()
+        forward(1, 0)
+
+    half_way = parts // 2
+    products(0, parts, 0, 1, [(parts - 2, early), (parts - 1, lambda: forward(1, 1))])
+    for copy in g_second:
+        copy.wait_recv()
+    products(parts, parts + half_way, 1, 3, [(parts + half_way - 1, lambda: forward(2, 0))])
+    for copy in g_third:
+        copy.wait_recv()
+    products(parts + half_way, 2 * parts, 1, 4, [(parts + half_way, lambda: forward(2, 1))])
+    products(2 * parts, 2 * parts + half_way, 3, 4, [(2 * parts, lambda: forward(3, 0))])
+
+    @pl.when(z == 0)
+    def _():
+        dn_ref[...] = jnp.zeros_like(dn_ref)
+
+    @pl.when(z == chips - 1)
+    def _():
+        up_ref[...] = jnp.zeros_like(up_ref)
+
+    def drain(slot, carry):
+        settle(slot)
+        return carry
+
+    first_slot = 2 * parts + half_way
+    lax.fori_loop(first_slot, first_slot + LEVEL_LAG, drain, 0)
+    forward(3, 1)
+    lax.fori_loop(first_slot + LEVEL_LAG, first_slot + 1 + LEVEL_LAG * (chips - 2), drain, 0)
+
+    for copy in g_first + g_second + g_third:
+        copy.wait_send()
+    for chip in range(chips):
+        for p in range(pieces):
+            to_up, to_dn, to_mate = block_copies(chip, p)
+            to_mate.wait()
+
+            @pl.when((z >= chip) & (z < chips - 1))
+            def _():
+                to_up.wait_send()
+
+            @pl.when((z <= chip) & (z > 0))
+            def _():
+                to_dn.wait_send()
+
+    def sent(j, carry):
+        dest = exclusive_or(r, j, rows_n)
+        for h in range(parts):
+            pair_copy(j, h).wait_send()
+
+            @pl.when(dest > z + 1)
+            def _():
+                up_copy(j, h).wait_send()
+
+            @pl.when(dest < z - 1)
+            def _():
+                dn_copy(j, h).wait_send()
+        return carry
+
+    lax.fori_loop(0, rows_n, sent, 0)
+
+
+def outer_kernel(x_ref, g_ref, out_ref, buf, sem):
+    slots, block, _ = buf.shape
+    steps = out_ref.shape[0] // block
+
+    def rows(i):
+        return pl.ds(pl.multiple_of(i * block, block), block)
+
+    def out_copy(i):
+        slot = lax.rem(i, slots)
+        return pltpu.make_async_copy(buf.at[slot], out_ref.at[rows(i)], sem.at[slot])
+
+    def body(i, carry):
+        @pl.when(i >= slots)
+        def _():
+            out_copy(i - slots).wait()
+
+        buf[lax.rem(i, slots), :, :] = lax.dot_general(
+            x_ref[:, rows(i)], g_ref[...], (((0,), (0,)), ((), ())), preferred_element_type=jnp.float32
+        )
+        out_copy(i).start()
+        return carry
+
+    lax.fori_loop(0, steps, body, 0)
+    for i in range(steps - slots, steps):
+        out_copy(i).wait()
+
+
+def outer_streamed(left, right):
+    tokens, depth = left.shape
+    width = right.shape[1]
+    block, slots = 2 * HEAD, 4
+    vmem = pl.BlockSpec(memory_space=pltpu.VMEM)
+    return pl.pallas_call(
+        outer_kernel,
+        out_shape=jax.ShapeDtypeStruct((depth, width), jnp.float32),
+        in_specs=[vmem, vmem],
+        out_specs=pl.BlockSpec(memory_space=pltpu.HBM),
+        scratch_shapes=[pltpu.VMEM((slots, block, width), jnp.float32), pltpu.SemaphoreType.DMA((slots,))],
+        compiler_params=pltpu.CompilerParams(vmem_limit_bytes=24 * 2**20),
+        cost_estimate=pl.CostEstimate(
+            flops=2 * tokens * depth * width, bytes_accessed=4 * depth * width, transcendentals=0
+        ),
+    )(left, right)
+
+
+def staged(rows_n, chips, inputs, weight, grad_out, positions):
+    depth, width = weight.shape
+    trow, tcol = grad_out.shape[0], inputs.shape[0]
+    parts = 4
+    dma = pltpu.SemaphoreType.DMA
+    vmem = pl.BlockSpec(memory_space=pltpu.VMEM)
+    hbm = pl.BlockSpec(memory_space=pltpu.HBM)
+    whole_grad, whole_inputs, own, upward, downward = pl.pallas_call(
+        functools.partial(staged_kernel, rows_n, chips, parts),
+        out_shape=(
+            jax.ShapeDtypeStruct((rows_n * trow, width), half),
+            jax.ShapeDtypeStruct((chips * 2 * tcol, depth), half),
+            jax.ShapeDtypeStruct((tcol, depth), jnp.float32),
+            jax.ShapeDtypeStruct((tcol, depth), half),
+            jax.ShapeDtypeStruct((tcol, depth), half),
+        ),
+        in_specs=[hbm, vmem, hbm, hbm],
+        out_specs=(vmem,) * 5,
+        scratch_shapes=[
+            pltpu.VMEM((depth, width), half),
+            pltpu.VMEM((trow, width), half),
+            pltpu.VMEM((2, rows_n, tcol, depth), half),
+            pltpu.VMEM((rows_n, tcol, depth), half),
+            pltpu.VMEM((rows_n, tcol, depth), half),
+            pltpu.VMEM((rows_n, tcol, depth), half),
+            pltpu.VMEM((rows_n, tcol, depth), half),
+            pltpu.VMEM((rows_n, tcol, depth), half),
+            dma((parts,)), dma((3,)),
+            dma((rows_n, 2)), dma((rows_n, 2)),
+            dma((chips, 2)), dma((chips, 2)), dma((chips, 2)), dma((chips, 2)), dma((chips, 2)),
+            dma((rows_n, parts)), dma((rows_n, parts)),
+            dma((rows_n, parts)), dma((rows_n, parts)), dma((rows_n, parts)), dma((rows_n, parts)),
+        ],
+        compiler_params=pltpu.CompilerParams(
+            collective_id=0, has_side_effects=True, vmem_limit_bytes=44 * 2**20
+        ),
+        cost_estimate=pl.CostEstimate(
+            flops=2 * rows_n * trow * width * depth, bytes_accessed=2 * width * depth, transcendentals=0
+        ),
+    )(grad_out, positions[None, :], inputs, weight)
+    cols = 2 * chips
+    from_below = lax.ppermute(upward, "col", [(q, q + 2) for q in range(cols - 2)])
+    from_above = lax.ppermute(downward, "col", [(q + 2, q) for q in range(cols - 2)])
+    weight_grad = outer_streamed(whole_inputs, whole_grad)
+    input_grad = (own + from_below.astype(jnp.float32) + from_above.astype(jnp.float32)).astype(half)
+    return (input_grad, weight_grad)
+
+
 def outer_sum(left, right):
     return lax.dot_general(
         left, right, (((0,), (0,)), ((), ())), preferred_element_type=jnp.float32
@@ -361,13 +755,14 @@
 def per_device(rows_n, chips, inputs, weight, grad_out, positions):
     depth, width = weight.shape
     trow, tcol = grad_out.shape[0], inputs.shape[0]
+    if rows_n == 4 and chips == 4 and width % (2 * HEAD) == 0 and depth % (8 * HEAD) == 0 and trow == 2 * tcol:
+        return staged(rows_n, chips, inputs, weight, grad_out, positions)
     col_start = lax.axis_index("col") * width
     raw = width % HEAD == 0
     grad = grad_out if raw else unrotate(grad_out, positions, col_start)
     parts = 8 if depth % (8 * HEAD) == 0 else 4
     dma = pltpu.SemaphoreType.DMA
     vmem = pl.BlockSpec(memory_space=pltpu.VMEM)
-    half = jnp.bfloat16
     whole_grad, whole_inputs, input_grad = pl.pallas_call(
         functools.partial(kernel, rows_n, chips, parts, raw),
         out_shape=(

time: 68.9 us -> 56.9 us (0.83)
  the two profiles are of different devices: /device:TPU:0 before, /device:TPU:14 now
where the time goes in v1:
time: 56.9 us; the launch traced here: 56.7 us
  Pallas kernels  46.8 us (82%)
  starting transfers between devices  5.85 us (10%)
  local copies, waits for them, and re-layouts  2.56 us (4%)
  other arithmetic  0.8 us (1%)
  between operations  0.69 us (1%)
    pallas_call x1, Pallas kernels, staged(): pl.pallas_call(functools.partial(staged_kernel, rows_n, chips, parts), ou...  34 us
    pallas_call x1, Pallas kernels, outer_streamed(): pl.pallas_call(outer_kernel, out_shape=jax.ShapeDtypeStruct((depth, width...  12.7 us
    ppermute x1, starting transfers between devices, staged(): lax.ppermute(downward, 'col', [(q + 2, q) for q in range(cols - 2)])  3.93 us
    unnamed x6, local copies, waits for them, and re-layouts  2.56 us
    ppermute x1, starting transfers between devices, staged(): lax.ppermute(upward, 'col', [(q, q + 2) for q in range(cols - 2)])  1.92 us
  transfers between devices with their start and end apart: 2, of which 0 were waited for; matrix products, arithmetic and copies ran while one was open for 0% of the time, Pallas kernels for 22%

profile of v1, /device:TPU:14, one launch (start us, length us, event | category | flops | bytes accessed | tf_op | source)
XLA Modules:
  0.0 56.7 jit_solution(2426924869332450717)
XLA Ops:
  0.6 0.0 copy-start
  0.6 1.0 %copy-done = bf16[64,2304]{1,0:T(8,128)(2,1)S(1)} copy-done((bf16[64,2304]{1,0:T(8,128)(2,1)S(1)}, bf16[64,2304]{1,0:T(8,128)(2,1)}, u32[]{:S(2)}) %copy-start) | copy-done | bytes 294936
  1.6 0.0 copy-start.1
  1.6 0.9 %copy-done.1 = bf16[32,4096]{1,0:T(8,128)(2,1)S(1)} copy-done((bf16[32,4096]{1,0:T(8,128)(2,1)S(1)}, bf16[32,4096]{1,0:T(8,128)(2,1)}, u32[]{:S(2)}) %copy-start.1) | copy-done | bytes 262168
  2.5 0.0 copy-start.2
  2.5 0.7 %copy-done.2 = s32[64]{0:T(128)S(1)} copy-done((s32[64]{0:T(128)S(1)}, s32[64]{0:T(128)}, u32[]{:S(2)}) %copy-start.2) | copy-done | bytes 280
  3.2 34.0 %shard_map.59 = (bf16[256,2304]{1,0:T(8,128)(2,1)S(1)}, bf16[256,4096]{1,0:T(8,128)(2,1)S(1)}, f32[32,4096]{1,0:T(8,128)S(1)}, bf16[32,4096]{1,0:T(8,128)(2,1)S(1)}, bf16[32,4096]{1,0:T(8,128)(2,1)S(1)}) custom-call(bf16[64,2304]{1,0:T(8,128)(2,1)S(1)} %copy-done, s32[1,64]{1,0:T(1,128)S(1)} %bitcast.1, bf16[32,4096]{1,0:T(8,128)(2,1)S(1)} %copy-done.1, ...), custom_call_target="tpu_custom_call" | custom-call | flops 4831838208 | bytes 18874368 | tf_op jit(solution)/shard_map/pallas_call | solution.py:708
  37.2 1.9 %collective-permute-start = (bf16[32,4096]{1,0:T(8,128)(2,1)S(1)}, bf16[32,4096]{1,0:T(8,128)(2,1)S(1)}, u32[]{:S(2)}, u32[]{:S(2)}) collective-permute-start(bf16[32,4096]{1,0:T(8,128)(2,1)S(1)} %get-tuple-element.8), channel_id=1, source_target_pairs={{0,2},{1,3},{2,4},{3,5},{4,6},{5,7},{8,10},{9,11},{10,12},{11,13},... | collective-permute-start | bytes 786440 | tf_op jit(solution)/shard_map/ppermute | solution.py:742
  39.2 3.9 %collective-permute-start.1 = (bf16[32,4096]{1,0:T(8,128)(2,1)S(1)}, bf16[32,4096]{1,0:T(8,128)(2,1)S(1)}, u32[]{:S(2)}, u32[]{:S(2)}) collective-permute-start(bf16[32,4096]{1,0:T(8,128)(2,1)S(1)} %get-tuple-element.9), channel_id=1, source_target_pairs={{2,0},{3,1},{4,2},{5,3},{6,4},{7,5},{10,8},{11,9},{12,10},{13,11},... | collective-permute-start | bytes 786440 | tf_op jit(solution)/shard_map/ppermute | solution.py:743
  43.1 12.7 %shard_map.60 = f32[4096,2304]{1,0:T(8,128)} custom-call(bf16[256,4096]{1,0:T(8,128)(2,1)S(1)} %get-tuple-element.10.x_ref, bf16[256,2304]{1,0:T(8,128)(2,1)S(1)} %get-tuple-element.11.g_ref), custom_call_target="tpu_custom_call" | custom-call | flops 4831838208 | bytes 37748736 | tf_op jit(solution)/shard_map/pallas_call | solution.py:688
  55.9 0.0 collective-permute-done
  55.9 0.0 collective-permute-done.1
  55.9 0.8 %add_convert_fusion = bf16[32,4096]{1,0:T(8,128)(2,1)} fusion(bf16[32,4096]{1,0:T(8,128)(2,1)S(1)} %collective-permute-done.1, f32[32,4096]{1,0:T(8,128)S(1)} %get-tuple-element.7, bf16[32,4096]{1,0:T(8,128)(2,1)S(1)} %collective-permute-done), kind=kLoop, calls=%fused_computation | loop fusion | flops 655360 | bytes 1310720 | tf_op jit(solution)/shard_map/convert_element_type | solution.py:745
Async XLA Ops:
  0.6 1.0 %copy-start = (bf16[64,2304]{1,0:T(8,128)(2,1)S(1)}, bf16[64,2304]{1,0:T(8,128)(2,1)}, u32[]{:S(2)}) copy-start(bf16[64,2304]{1,0:T(8,128)(2,1)} %g_hbm.1) | copy-start | bytes 884740
  1.6 0.9 %copy-start.1 = (bf16[32,4096]{1,0:T(8,128)(2,1)S(1)}, bf16[32,4096]{1,0:T(8,128)(2,1)}, u32[]{:S(2)}) copy-start(bf16[32,4096]{1,0:T(8,128)(2,1)} %x_hbm.1) | copy-start | bytes 786436
  2.5 0.7 %copy-start.2 = (s32[64]{0:T(128)S(1)}, s32[64]{0:T(128)}, u32[]{:S(2)}) copy-start(s32[64]{0:T(128)} %param.7) | copy-start | bytes 772
  37.2 18.6 %collective-permute-start = (bf16[32,4096]{1,0:T(8,128)(2,1)S(1)}, bf16[32,4096]{1,0:T(8,128)(2,1)S(1)}, u32[]{:S(2)}, u32[]{:S(2)}) collective-permute-start(bf16[32,4096]{1,0:T(8,128)(2,1)S(1)} %get-tuple-element.8), channel_id=1, source_target_pairs={{0,2},{1,3},{2,4},{3,5},{4,6},{5,7},{8,10},{9,11},{10,12},{11,13},... | collective-permute-start | bytes 786440 | tf_op jit(solution)/shard_map/ppermute | solution.py:742
  39.2 16.7 %collective-permute-start.1 = (bf16[32,4096]{1,0:T(8,128)(2,1)S(1)}, bf16[32,4096]{1,0:T(8,128)(2,1)S(1)}, u32[]{:S(2)}, u32[]{:S(2)}) collective-permute-start(bf16[32,4096]{1,0:T(8,128)(2,1)S(1)} %get-tuple-element.9), channel_id=1, source_target_pairs={{2,0},{3,1},{4,2},{5,3},{6,4},{7,5},{10,8},{11,9},{12,10},{13,11},... | collective-permute-start | bytes 786440 | tf_op jit(solution)/shard_map/ppermute | solution.py:743

commit v2 on v1

--- a/solution.py
+++ b/solution.py
@@ -13,6 +13,7 @@
 HEAD = 128
 PAIR_LAG = 2
 LEVEL_LAG = 3
+CHAIN_LAG = 3
 MESH = pl.DeviceIdType.MESH
 half = jnp.bfloat16
 
@@ -353,14 +354,20 @@
                 dn_copy(chip, h).wait_send()
 
 
-def staged_kernel(rows_n, chips, parts, g_hbm, pos_ref, x_hbm, w_ref, gall, xall, own_ref, up_ref, dn_ref,
-                  w_v, raw, pb, rb, ub, db, sb_up, sb_dn,
+def is_rising(row):
+    return row // 2 % 2 == 0
+
+
+def staged_kernel(rows_n, chips, parts, g_hbm, pos_hbm, x_hbm, w_ref, gall, xall, own_ref, last_ref,
+                  w_v, raw, pos_ref, pb, rb, ub, db, sb_up, sb_dn,
                   w_sem, in_sem, gs, gr, xs_up, xs_dn, xs_p, xr, xp, ps, pr, us, ur, ds, dr):
     r = lax.axis_index("row")
     q = lax.axis_index("col")
     z, c = q // 2, q % 2
     mate = z * 2 + 1 - c
     up, down = q + 2, q - 2
+    rising = is_rising(r)
+    falling = jnp.logical_not(rising)
     trow, width = g_hbm.shape
     tcol, depth = x_hbm.shape
     dc = depth // parts
@@ -373,6 +380,8 @@
 
     g_in = pltpu.make_async_copy(g_hbm, raw, in_sem.at[0])
     g_in.start()
+    pos_in = pltpu.make_async_copy(pos_hbm, pos_ref, in_sem.at[3])
+    pos_in.start()
     x_in = [pltpu.make_async_copy(x_hbm.at[pl.ds(p * prow, prow)], xall.at[x_rows(z, c, p)], in_sem.at[1 + p])
             for p in range(pieces)]
     for copy in x_in:
@@ -398,6 +407,7 @@
     for h in range(parts):
         w_copy(h).start()
 
+    pos_in.wait()
     g_in.wait()
     unrotate_heads(raw, pos_ref, gall, q * width)
     for copy in x_in:
@@ -508,73 +518,121 @@
         for j in range(first, last):
             pair_copy(j, h).start()
 
-    def each_block(i, act):
-        def body(j, carry):
-            least = parts * ((j + 3) // 4) + (parts // 2) * (j // 3)
-
-            @pl.when((i >= least) & (i < least + parts))
-            def _():
-                act(j, (i + 4 * LEVEL_LAG * parts) % parts, exclusive_or(r, j, rows_n))
-
-            return carry
-
-        lax.fori_loop(0, rows_n, body, 0)
+    count = 2 * parts + parts // 2
+    firsts = [parts * ((j + 3) // 4) + (parts // 2) * (j // 3) for j in range(rows_n)]
+
+    def each_block(slot, lo, hi, lag, act, busy=None, late=None):
+        def block(j, guard=None):
+            least, most = firsts[j], firsts[j] + parts
+            if hi - lag <= least or lo - lag >= most:
+                return
+            dest = exclusive_or(r, j, rows_n)
+
+            def run():
+                act(j, (slot - lag) % parts, dest)
+
+            conds = [] if guard is None else [guard(dest)]
+            if lo - lag < least or hi - lag > most:
+                conds.append((slot - lag >= least) & (slot - lag < most))
+            if conds:
+                pl.when(functools.reduce(jnp.logical_and, conds))(run)
+            else:
+                run()
+
+        last_parts = late is not None and hi - lag > count - parts
+
+        if busy is not False:
+            block(3, (lambda dest: dest != late) if last_parts else None)
+            block(2, (lambda dest: (dest != late) | (slot - lag < count - parts)) if last_parts else None)
+        block(1)
+        block(0)
+        if last_parts:
+            block(3, lambda dest: dest == late)
 
     def own_step(j, h, dest):
         pair_copy(j, h).wait_recv()
 
-        @pl.when(dest == z)
-        def _():
-            own_ref[:, part(h)] = pair_sum(j, h)
-
-    def up_step(j, h, dest):
-        copy = up_copy(j, h)
-
-        def finish(total):
-            @pl.when(dest == z + 1)
-            def _():
-                up_ref[:, part(h)] = total.astype(half)
-
-            @pl.when(dest > z + 1)
-            def _():
-                sb_up[j, :, part(h)] = total.astype(half)
-                copy.start()
-
-        @pl.when((dest > z) & (z == 0))
-        def _():
-            finish(pair_sum(j, h))
-
-        @pl.when((dest > z) & (z > 0))
+    def chain_step(copy, arrived, sent, busy, ends, origin, near, beyond, here, h, j):
+        def total():
+            return pair_sum(j, h)
+
+        sends, stays = (beyond, near) if busy else (beyond | near, here)
+
+        def settled(value):
+            if ends is not True:
+                @pl.when(sends)
+                def _():
+                    sent[j, :, part(h)] = value.astype(half)
+                    copy.start()
+
+            if ends is not False:
+                @pl.when(stays)
+                def _():
+                    if busy:
+                        last_ref[:, part(h)] = value.astype(half)
+                    else:
+                        own_ref[:, part(h)] = value
+
+        takes = sends | stays if ends is None else stays if ends else sends
+
+        @pl.when(takes & jnp.logical_not(origin))
         def _():
             copy.wait_recv()
-            finish(pair_sum(j, h) + ub[j, :, part(h)].astype(jnp.float32))
-
-    def dn_step(j, h, dest):
-        copy = dn_copy(j, h)
-
-        def finish(total):
-            @pl.when(dest == z - 1)
-            def _():
-                dn_ref[:, part(h)] = total.astype(half)
-
-            @pl.when(dest < z - 1)
-            def _():
-                sb_dn[j, :, part(h)] = total.astype(half)
-                copy.start()
-
-        @pl.when((dest < z) & (z == chips - 1))
-        def _():
-            finish(pair_sum(j, h))
-
-        @pl.when((dest < z) & (z < chips - 1))
-        def _():
-            copy.wait_recv()
-            finish(pair_sum(j, h) + db[j, :, part(h)].astype(jnp.float32))
-
-    def settle(slot):
-        each_block(slot - 1, own_step)
-        each_block(slot - 1 - LEVEL_LAG * z, up_step)
-        each_block(slot - 1 - LEVEL_LAG * (chips - 1 - z), dn_step)
+            settled(total() + arrived[j, :, part(h)].astype(jnp.float32))
+
+        @pl.when((takes & origin))
+        def _():
+            settled(total())
+
+    def up_step(busy, ends, j, h, dest):
+        chain_step(up_copy(j, h), ub, sb_up, busy, ends, z == 0, dest == z + 1, dest > z + 1, dest == z, h, j)
+
+    def dn_step(busy, ends, j, h, dest):
+        chain_step(dn_copy(j, h), db, sb_dn, busy, ends, z == chips - 1, dest == z - 1, dest < z - 1, dest == z, h, j)
+
+    late_up, late_dn = 2, chips - 3
+
+    def settle_late(chip):
+        for busy, late, at, act in ((rising, late_up, chip, up_step), (falling, late_dn, chips - 1 - chip, dn_step)):
+            for i in range(count - parts, 2 * parts):
+                dest = exclusive_or(r, 2, rows_n)
+
+                @pl.when((z == at) & (dest == late) & busy)
+                def _():
+                    act(True, None, 2, i % parts, dest)
+
+    def settle_short(chip, products):
+        for idle, at, act in ((falling, chip, up_step), (rising, chips - 1 - chip, dn_step)):
+            @pl.when((z == at) & idle)
+            def _():
+                for i in products:
+                    for j in (2, 3):
+                        if firsts[j] <= i < firsts[j] + parts:
+                            act(False, None, j, i % parts, exclusive_or(r, j, rows_n))
+
+    def settle(slot, lo, hi, ends=None):
+        if not ends:
+            each_block(slot, lo, hi, 1, own_step)
+        for chip in range(chips):
+            lag_up, lag_dn = 1 + CHAIN_LAG * chip, 1 + CHAIN_LAG * (chips - 1 - chip)
+            ups = hi > lag_up and lo < count + lag_up
+            dns = hi > lag_dn and lo < count + lag_dn
+            if not (ups or dns):
+                continue
+
+            @pl.when((z == chip) & rising)
+            def _():
+                if dns:
+                    each_block(slot, lo, hi, lag_dn, functools.partial(dn_step, False, ends), False)
+                if ups:
+                    each_block(slot, lo, hi, lag_up, functools.partial(up_step, True, ends), True, late_up)
+
+            @pl.when((z == chip) & falling)
+            def _():
+                if ups:
+                    each_block(slot, lo, hi, lag_up, functools.partial(up_step, False, ends), False)
+                if dns:
+                    each_block(slot, lo, hi, lag_dn, functools.partial(dn_step, True, ends), True, late_dn)
 
     def products(start, stop, first, last, after):
         def body(i, carry):
@@ -583,7 +641,7 @@
             multiply(i, first, last)
             for at, act in after:
                 pl.when(i == at)(act)
-            settle(i)
+            settle(i, start, stop)
             return carry
 
         lax.fori_loop(start, stop, body, 0)
@@ -604,22 +662,21 @@
     products(parts + half_way, 2 * parts, 1, 4, [(parts + half_way, lambda: forward(2, 1))])
     products(2 * parts, 2 * parts + half_way, 3, 4, [(2 * parts, lambda: forward(3, 0))])
 
-    @pl.when(z == 0)
-    def _():
-        dn_ref[...] = jnp.zeros_like(dn_ref)
-
-    @pl.when(z == chips - 1)
-    def _():
-        up_ref[...] = jnp.zeros_like(up_ref)
-
-    def drain(slot, carry):
-        settle(slot)
-        return carry
-
-    first_slot = 2 * parts + half_way
-    lax.fori_loop(first_slot, first_slot + LEVEL_LAG, drain, 0)
-    forward(3, 1)
-    lax.fori_loop(first_slot + LEVEL_LAG, first_slot + 1 + LEVEL_LAG * (chips - 2), drain, 0)
+    @pl.when((rising & (z == chips - 1)) | (falling & (z == 0)))
+    def _():
+        last_ref[...] = jnp.zeros_like(last_ref)
+
+    settle_short(0, range(parts, count - 1))
+    for slot in range(count, count + 1 + CHAIN_LAG * (chips - 1)):
+        settle(slot, slot, slot + 1, False)
+        if slot == count:
+            forward(3, 1)
+            settle_short(0, [count - 1])
+            settle_late(0)
+    for slot in range(count, count + 1 + CHAIN_LAG * (chips - 1)):
+        settle(slot, slot, slot + 1, True)
+    settle_late(1)
+    settle_short(1, range(parts, count))
 
     for copy in g_first + g_second + g_third:
         copy.wait_send()
@@ -641,11 +698,11 @@
         for h in range(parts):
             pair_copy(j, h).wait_send()
 
-            @pl.when(dest > z + 1)
+            @pl.when((dest > z + 1) | (falling & (dest == z + 1)))
             def _():
                 up_copy(j, h).wait_send()
 
-            @pl.when(dest < z - 1)
+            @pl.when((dest < z - 1) | (rising & (dest == z - 1)))
             def _():
                 dn_copy(j, h).wait_send()
         return carry
@@ -705,27 +762,27 @@
     dma = pltpu.SemaphoreType.DMA
     vmem = pl.BlockSpec(memory_space=pltpu.VMEM)
     hbm = pl.BlockSpec(memory_space=pltpu.HBM)
-    whole_grad, whole_inputs, own, upward, downward = pl.pallas_call(
+    whole_grad, whole_inputs, own, last = pl.pallas_call(
         functools.partial(staged_kernel, rows_n, chips, parts),
         out_shape=(
             jax.ShapeDtypeStruct((rows_n * trow, width), half),
             jax.ShapeDtypeStruct((chips * 2 * tcol, depth), half),
             jax.ShapeDtypeStruct((tcol, depth), jnp.float32),
             jax.ShapeDtypeStruct((tcol, depth), half),
-            jax.ShapeDtypeStruct((tcol, depth), half),
         ),
-        in_specs=[hbm, vmem, hbm, hbm],
-        out_specs=(vmem,) * 5,
+        in_specs=[hbm] * 4,
+        out_specs=(vmem,) * 4,
         scratch_shapes=[
             pltpu.VMEM((depth, width), half),
             pltpu.VMEM((trow, width), half),
+            pltpu.VMEM((1, trow), jnp.int32),
             pltpu.VMEM((2, rows_n, tcol, depth), half),
             pltpu.VMEM((rows_n, tcol, depth), half),
             pltpu.VMEM((rows_n, tcol, depth), half),
             pltpu.VMEM((rows_n, tcol, depth), half),
             pltpu.VMEM((rows_n, tcol, depth), half),
             pltpu.VMEM((rows_n, tcol, depth), half),
-            dma((parts,)), dma((3,)),
+            dma((parts,)), dma((4,)),
             dma((rows_n, 2)), dma((rows_n, 2)),
             dma((chips, 2)), dma((chips, 2)), dma((chips, 2)), dma((chips, 2)), dma((chips, 2)),
             dma((rows_n, parts)), dma((rows_n, parts)),
@@ -737,12 +794,13 @@
         cost_estimate=pl.CostEstimate(
             flops=2 * rows_n * trow * width * depth, bytes_accessed=2 * width * depth, transcendentals=0
         ),
-    )(grad_out, positions[None, :], inputs, weight)
+    )(*(pltpu.with_memory_space_constraint(a, pltpu.HBM) for a in (grad_out, positions[None, :], inputs, weight)))
     cols = 2 * chips
-    from_below = lax.ppermute(upward, "col", [(q, q + 2) for q in range(cols - 2)])
-    from_above = lax.ppermute(downward, "col", [(q + 2, q) for q in range(cols - 2)])
+    hops = [(row * cols + q, row * cols + q + 2) for row in range(rows_n) for q in range(cols - 2)]
+    hops = [(a, b) if is_rising(a // cols) else (b, a) for a, b in hops]
+    arrived = lax.ppermute(last, ("row", "col"), hops)
     weight_grad = outer_streamed(whole_inputs, whole_grad)
-    input_grad = (own + from_below.astype(jnp.float32) + from_above.astype(jnp.float32)).astype(half)
+    input_grad = (own + arrived.astype(jnp.float32)).astype(half)
     return (input_grad, weight_grad)
 
 

time: 56.9 us -> 48.8 us (0.86)
  the two profiles are of different devices: /device:TPU:14 before, /device:TPU:0 now
where the time goes in v2:
time: 48.8 us; the launch traced here: 48.6 us
  Pallas kernels  42.9 us (88%)
  starting transfers between devices  4.26 us (9%)
  other arithmetic  0.75 us (2%)
  between operations  0.66 us (1%)
    pallas_call x1, Pallas kernels, staged(): pl.pallas_call(functools.partial(staged_kernel, rows_n, chips, parts), ou...  30.2 us
    pallas_call x1, Pallas kernels, outer_streamed(): pl.pallas_call(outer_kernel, out_shape=jax.ShapeDtypeStruct((depth, width...  12.7 us
    ppermute x1, starting transfers between devices, staged(): arrived = lax.ppermute(last, ('row', 'col'), hops)  4.26 us
  transfers between devices with their start and end apart: 1, of which 0 were waited for; matrix products, arithmetic and copies ran while one was open for 0% of the time, Pallas kernels for 26%

profile of v2, /device:TPU:0, one launch (start us, length us, event | category | flops | bytes accessed | tf_op | source)
XLA Modules:
  0.0 48.6 jit_solution(12376891841438219405)
XLA Ops:
  0.6 30.2 %shard_map.59 = (bf16[256,2304]{1,0:T(8,128)(2,1)S(1)}, bf16[256,4096]{1,0:T(8,128)(2,1)S(1)}, f32[32,4096]{1,0:T(8,128)S(1)}, bf16[32,4096]{1,0:T(8,128)(2,1)S(1)}) custom-call(bf16[64,2304]{1,0:T(8,128)(2,1)} %g_hbm.1, s32[1,64]{1,0:T(1,128)} %bitcast.1, bf16[32,4096]{1,0:T(8,128)(2,1)} %x_hbm.1, bf16[4096,2304]{1,0:T(8,128)(2,1)} %w_ref.1), custom_call_target="tpu_custom_call" | custom-call | flops 4831838208 | bytes 18874368 | tf_op jit(solution)/shard_map/pallas_call | solution.py:765
  30.8 4.3 %collective-permute-start = (bf16[32,4096]{1,0:T(8,128)(2,1)S(1)}, bf16[32,4096]{1,0:T(8,128)(2,1)S(1)}, u32[]{:S(2)}, u32[]{:S(2)}) collective-permute-start(bf16[32,4096]{1,0:T(8,128)(2,1)S(1)} %get-tuple-element.7), channel_id=1, source_target_pairs={{0,2},{1,3},{2,4},{3,5},{4,6},{5,7},{8,10},{9,11},{10,12},{11,13},... | collective-permute-start | bytes 786440 | tf_op jit(solution)/shard_map/ppermute | solution.py:801
  35.1 12.7 %shard_map.60 = f32[4096,2304]{1,0:T(8,128)} custom-call(bf16[256,4096]{1,0:T(8,128)(2,1)S(1)} %get-tuple-element.8.x_ref, bf16[256,2304]{1,0:T(8,128)(2,1)S(1)} %get-tuple-element.9.g_ref), custom_call_target="tpu_custom_call" | custom-call | flops 4831838208 | bytes 37748736 | tf_op jit(solution)/shard_map/pallas_call | solution.py:745
  47.8 0.0 collective-permute-done
  47.8 0.8 %add_convert_fusion = bf16[32,4096]{1,0:T(8,128)(2,1)} fusion(f32[32,4096]{1,0:T(8,128)S(1)} %get-tuple-element.6, bf16[32,4096]{1,0:T(8,128)(2,1)S(1)} %collective-permute-done), kind=kLoop, calls=%fused_computation | loop fusion | flops 393216 | bytes 1048576 | tf_op jit(solution)/shard_map/convert_element_type | solution.py:803
Async XLA Ops:
  30.8 17.0 %collective-permute-start = (bf16[32,4096]{1,0:T(8,128)(2,1)S(1)}, bf16[32,4096]{1,0:T(8,128)(2,1)S(1)}, u32[]{:S(2)}, u32[]{:S(2)}) collective-permute-start(bf16[32,4096]{1,0:T(8,128)(2,1)S(1)} %get-tuple-element.7), channel_id=1, source_target_pairs={{0,2},{1,3},{2,4},{3,5},{4,6},{5,7},{8,10},{9,11},{10,12},{11,13},... | collective-permute-start | bytes 786440 | tf_op jit(solution)/shard_map/ppermute | solution.py:801

commit v3 on v2

--- a/solution.py
+++ b/solution.py
@@ -14,6 +14,7 @@
 PAIR_LAG = 2
 LEVEL_LAG = 3
 CHAIN_LAG = 3
+NEAR_LAG = 2
 MESH = pl.DeviceIdType.MESH
 half = jnp.bfloat16
 
@@ -521,10 +522,10 @@
     count = 2 * parts + parts // 2
     firsts = [parts * ((j + 3) // 4) + (parts // 2) * (j // 3) for j in range(rows_n)]
 
-    def each_block(slot, lo, hi, lag, act, busy=None, late=None):
+    def each_block(slot, lo, hi, lag, act, busy=None, late=None, only=None):
         def block(j, guard=None):
             least, most = firsts[j], firsts[j] + parts
-            if hi - lag <= least or lo - lag >= most:
+            if hi - lag <= least or lo - lag >= most or only not in (None, j):
                 return
             dest = exclusive_or(r, j, rows_n)
 
@@ -610,27 +611,25 @@
                         if firsts[j] <= i < firsts[j] + parts:
                             act(False, None, j, i % parts, exclusive_or(r, j, rows_n))
 
-    def settle(slot, lo, hi, ends=None):
-        if not ends:
+    def settle(slot, lo, hi, ends=None, pairs=True, chain=None):
+        if pairs and not ends:
             each_block(slot, lo, hi, 1, own_step)
-        for chip in range(chips):
+        for chip in range(chips) if chain is None else chain:
             lag_up, lag_dn = 1 + CHAIN_LAG * chip, 1 + CHAIN_LAG * (chips - 1 - chip)
+            near_up, near_dn = 1 + NEAR_LAG * chip, 1 + NEAR_LAG * (chips - 1 - chip)
             ups = hi > lag_up and lo < count + lag_up
             dns = hi > lag_dn and lo < count + lag_dn
-            if not (ups or dns):
-                continue
-
             @pl.when((z == chip) & rising)
             def _():
-                if dns:
-                    each_block(slot, lo, hi, lag_dn, functools.partial(dn_step, False, ends), False)
+                for j, lag in ((1, near_dn), (0, lag_dn)):
+                    each_block(slot, lo, hi, lag, functools.partial(dn_step, False, ends), False, only=j)
                 if ups:
                     each_block(slot, lo, hi, lag_up, functools.partial(up_step, True, ends), True, late_up)
 
             @pl.when((z == chip) & falling)
             def _():
-                if ups:
-                    each_block(slot, lo, hi, lag_up, functools.partial(up_step, False, ends), False)
+                for j, lag in ((1, near_up), (0, lag_up)):
+                    each_block(slot, lo, hi, lag, functools.partial(up_step, False, ends), False, only=j)
                 if dns:
                     each_block(slot, lo, hi, lag_dn, functools.partial(dn_step, True, ends), True, late_dn)
 
@@ -668,16 +667,15 @@
 
     settle_short(0, range(parts, count - 1))
     for slot in range(count, count + 1 + CHAIN_LAG * (chips - 1)):
-        settle(slot, slot, slot + 1, False)
         if slot == count:
+            settle(slot, slot, slot + 1, False, False, range(1, chips - 1))
+            settle(slot, slot, slot + 1, False, True, (0, chips - 1))
             forward(3, 1)
+        else:
+            settle(slot, slot, slot + 1, False)
+        if slot == count:
             settle_short(0, [count - 1])
             settle_late(0)
-    for slot in range(count, count + 1 + CHAIN_LAG * (chips - 1)):
-        settle(slot, slot, slot + 1, True)
-    settle_late(1)
-    settle_short(1, range(parts, count))
-
     for copy in g_first + g_second + g_third:
         copy.wait_send()
     for chip in range(chips):
@@ -693,11 +691,21 @@
             def _():
                 to_dn.wait_send()
 
+    def swapped(j, carry):
+        for h in range(parts):
+            pair_copy(j, h).wait_send()
+        return carry
+
+    lax.fori_loop(0, rows_n, swapped, 0)
+
+    for slot in range(count, count + 1 + CHAIN_LAG * (chips - 1)):
+        settle(slot, slot, slot + 1, True)
+    settle_late(1)
+    settle_short(1, range(parts, count))
+
     def sent(j, carry):
         dest = exclusive_or(r, j, rows_n)
         for h in range(parts):
-            pair_copy(j, h).wait_send()
-
             @pl.when((dest > z + 1) | (falling & (dest == z + 1)))
             def _():
                 up_copy(j, h).wait_send()

time: 48.8 us -> 48.7 us (level)
  no operation moved by 1% of the time
where the time goes in v3:
time: 48.7 us; the launch traced here: 48.5 us
  Pallas kernels  42.8 us (88%)
  starting transfers between devices  4.31 us (9%)
  other arithmetic  0.75 us (2%)
  between operations  0.66 us (1%)
    pallas_call x1, Pallas kernels, staged(): pl.pallas_call(functools.partial(staged_kernel, rows_n, chips, parts), ou...  30.1 us
    pallas_call x1, Pallas kernels, outer_streamed(): pl.pallas_call(outer_kernel, out_shape=jax.ShapeDtypeStruct((depth, width...  12.7 us
    ppermute x1, starting transfers between devices, staged(): arrived = lax.ppermute(last, ('row', 'col'), hops)  4.31 us
  transfers between devices with their start and end apart: 1, of which 0 were waited for; matrix products, arithmetic and copies ran while one was open for 0% of the time, Pallas kernels for 26%

profile of v3, /device:TPU:0, one launch (start us, length us, event | category | flops | bytes accessed | tf_op | source)
XLA Modules:
  0.0 48.5 jit_solution(15784925747643103367)
XLA Ops:
  0.6 30.1 %shard_map.59 = (bf16[256,2304]{1,0:T(8,128)(2,1)S(1)}, bf16[256,4096]{1,0:T(8,128)(2,1)S(1)}, f32[32,4096]{1,0:T(8,128)S(1)}, bf16[32,4096]{1,0:T(8,128)(2,1)S(1)}) custom-call(bf16[64,2304]{1,0:T(8,128)(2,1)} %g_hbm.1, s32[1,64]{1,0:T(1,128)} %bitcast.1, bf16[32,4096]{1,0:T(8,128)(2,1)} %x_hbm.1, bf16[4096,2304]{1,0:T(8,128)(2,1)} %w_ref.1), custom_call_target="tpu_custom_call" | custom-call | flops 4831838208 | bytes 18874368 | tf_op jit(solution)/shard_map/pallas_call | solution.py:773
  30.7 4.3 %collective-permute-start = (bf16[32,4096]{1,0:T(8,128)(2,1)S(1)}, bf16[32,4096]{1,0:T(8,128)(2,1)S(1)}, u32[]{:S(2)}, u32[]{:S(2)}) collective-permute-start(bf16[32,4096]{1,0:T(8,128)(2,1)S(1)} %get-tuple-element.7), channel_id=1, source_target_pairs={{0,2},{1,3},{2,4},{3,5},{4,6},{5,7},{8,10},{9,11},{10,12},{11,13},... | collective-permute-start | bytes 786440 | tf_op jit(solution)/shard_map/ppermute | solution.py:809
  35.0 12.7 %shard_map.60 = f32[4096,2304]{1,0:T(8,128)} custom-call(bf16[256,4096]{1,0:T(8,128)(2,1)S(1)} %get-tuple-element.8.x_ref, bf16[256,2304]{1,0:T(8,128)(2,1)S(1)} %get-tuple-element.9.g_ref), custom_call_target="tpu_custom_call" | custom-call | flops 4831838208 | bytes 37748736 | tf_op jit(solution)/shard_map/pallas_call | solution.py:753
  47.8 0.0 collective-permute-done
  47.8 0.8 %add_convert_fusion = bf16[32,4096]{1,0:T(8,128)(2,1)} fusion(f32[32,4096]{1,0:T(8,128)S(1)} %get-tuple-element.6, bf16[32,4096]{1,0:T(8,128)(2,1)S(1)} %collective-permute-done), kind=kLoop, calls=%fused_computation | loop fusion | flops 393216 | bytes 1048576 | tf_op jit(solution)/shard_map/convert_element_type | solution.py:811
Async XLA Ops:
  30.7 17.1 %collective-permute-start = (bf16[32,4096]{1,0:T(8,128)(2,1)S(1)}, bf16[32,4096]{1,0:T(8,128)(2,1)S(1)}, u32[]{:S(2)}, u32[]{:S(2)}) collective-permute-start(bf16[32,4096]{1,0:T(8,128)(2,1)S(1)} %get-tuple-element.7), channel_id=1, source_target_pairs={{0,2},{1,3},{2,4},{3,5},{4,6},{5,7},{8,10},{9,11},{10,12},{11,13},... | collective-permute-start | bytes 786440 | tf_op jit(solution)/shard_map/ppermute | solution.py:809
